TPU v7x, 8 devices: a whole 2x2x1 slice. The times are simulated.
8 devices in a mesh: dp: 1 (over z), heads: 2 (over y), ctx: 4 (over x, core).
Axes of the slice: x: 2, y: 2, z: 1, core: 2. Of those that a mesh axis runs over, the one named last changes fastest.
Arguments:
- hidden: bfloat16 [256, 2304], P(('dp', 'ctx'))
- w_query: bfloat16 [2304, 2048], P(None, 'heads')
- w_key: bfloat16 [2304, 1024], P(None, 'heads')
- w_value: bfloat16 [2304, 1024], P(None, 'heads')
- w_out: bfloat16 [2048, 2304], P('heads')
- prefix_k: bfloat16 [4096, 4, 256], P(('dp', 'ctx'), 'heads')
- prefix_v: bfloat16 [4096, 4, 256], P(('dp', 'ctx'), 'heads')
- suffix_k: bfloat16 [256, 512, 4, 256], P(('dp', 'ctx'), None, 'heads')
- suffix_v: bfloat16 [256, 512, 4, 256], P(('dp', 'ctx'), None, 'heads')
- seq_lens: int32 [256], P(('dp', 'ctx'))
Outputs:
- output: bfloat16 [256, 2304], P(('dp', 'ctx'))
All inputs are finite; a program needn't handle non-finite values.
Results may differ from a plain program's by a relative error of at most 0.00434775.
Values are sent between devices in bfloat16 or wider.
A program may use at most 1 GiB of HBM per device.

v0:
```python
import functools
import jax
import jax.numpy as jnp
from jax import lax
from jax.sharding import PartitionSpec as P


def prefix_state(q_block, pre_k, pre_v):
    score_scale = q_block.shape[-1] ** -0.5
    scores = jnp.einsum('bkgd,pkd->bkgp', q_block, pre_k, preferred_element_type=jnp.float32) * score_scale
    row_max = jnp.max(scores, axis=-1)
    weights = jnp.exp(scores - row_max[..., None])
    weight_sum = jnp.sum(weights, axis=-1)
    summed = jnp.einsum('bkgp,pkd->bkgd', weights.astype(jnp.bfloat16), pre_v, preferred_element_type=jnp.float32)
    return summed / weight_sum[..., None], row_max + jnp.log(weight_sum)


def suffix_state(queries, key_new, val_new, suf_k, suf_v, seq_lens):
    score_scale = queries.shape[-1] ** -0.5
    cached = jnp.einsum('bkgd,bskd->bkgs', queries, suf_k, preferred_element_type=jnp.float32) * score_scale
    slot_ids = jnp.arange(suf_k.shape[1])
    in_range = (slot_ids[None, :] < seq_lens[:, None])[:, None, None, :]
    cached = jnp.where(in_range, cached, -jnp.inf)
    new_score = jnp.einsum('clhe,cle->clh', queries, key_new, preferred_element_type=jnp.float32) * score_scale
    row_max = jnp.maximum(jnp.max(cached, axis=-1), new_score)
    w_cached = jnp.exp(cached - row_max[..., None])
    w_fresh = jnp.exp(new_score - row_max)
    weight_sum = jnp.sum(w_cached, axis=-1) + w_fresh
    summed = jnp.einsum('bkgs,bskd->bkgd', w_cached.astype(jnp.bfloat16), suf_v, preferred_element_type=jnp.float32)
    summed = summed + jnp.einsum('clh,cle->clhe', w_fresh.astype(jnp.bfloat16), val_new, preferred_element_type=jnp.float32)
    return summed / weight_sum[..., None], row_max + jnp.log(weight_sum)


def merge_states(pre_out, pre_lse, suf_out, suf_lse):
    all_max = jnp.maximum(jnp.max(pre_lse, axis=0), suf_lse)
    pre_w = jnp.exp(pre_lse - all_max)
    suf_w = jnp.exp(suf_lse - all_max)
    norm_sum = jnp.sum(pre_w, axis=0) + suf_w
    merged = jnp.sum(pre_w[..., None] * pre_out, axis=0) + suf_w[..., None] * suf_out
    return merged / norm_sum[..., None]


def solution(mesh):
    row_spec = P(('dp', 'ctx'), None)
    col_spec = P(None, 'heads')
    pre_spec = P(('dp', 'ctx'), 'heads', None)
    suf_spec = P(('dp', 'ctx'), None, 'heads', None)

    def local_step(hidden, w_query, w_key, w_value, w_out, prefix_k, prefix_v, suffix_k, suffix_v, seq_lens):
        n_rows = hidden.shape[0]
        kv_local = prefix_k.shape[1]
        head_dim = prefix_k.shape[2]
        q_group = w_query.shape[1] // (kv_local * head_dim)
        queries = jnp.dot(hidden, w_query, preferred_element_type=jnp.float32).astype(jnp.bfloat16).reshape(n_rows, kv_local, q_group, head_dim)
        key_new = jnp.dot(hidden, w_key, preferred_element_type=jnp.float32).astype(jnp.bfloat16).reshape(n_rows, kv_local, head_dim)
        val_new = jnp.dot(hidden, w_value, preferred_element_type=jnp.float32).astype(jnp.bfloat16).reshape(n_rows, kv_local, head_dim)
        all_queries = lax.all_gather(queries, 'ctx', axis=0)
        pre_out, pre_lse = lax.map(functools.partial(prefix_state, pre_k=prefix_k, pre_v=prefix_v), all_queries)
        pre_out = lax.all_to_all(pre_out, 'ctx', 0, 0, tiled=True)
        pre_lse = lax.all_to_all(pre_lse, 'ctx', 0, 0, tiled=True)
        suf_out, suf_lse = suffix_state(queries, key_new, val_new, suffix_k, suffix_v, seq_lens)
        merged = merge_states(pre_out, pre_lse, suf_out, suf_lse)
        attended = merged.astype(jnp.bfloat16).reshape(n_rows, kv_local * q_group * head_dim)
        partial_y = jnp.dot(attended, w_out, preferred_element_type=jnp.float32)
        summed_y = lax.psum(partial_y, 'heads')
        return (hidden.astype(jnp.float32) + summed_y).astype(jnp.bfloat16)

    return jax.shard_map(local_step, mesh=mesh, in_specs=(row_spec, col_spec, col_spec, col_spec, P('heads', None), pre_spec, pre_spec, suf_spec, suf_spec, P(('dp', 'ctx'))), out_specs=row_spec, check_vma=False)
```

profile of v0, /device:TPU:0, one launch (start us, length us, event | category | flops | bytes accessed | tf_op | source)
XLA Modules:
  0.0 139.8 jit_solution(4169409656140901167)
XLA Ops:
  6.5 0.0 copy-start
  6.5 3.5 %convolution_convert_fusion = bf16[64,1024]{1,0:T(8,128)(2,1)S(1)} fusion(bf16[64,2304]{1,0:T(8,128)(2,1)} %param.12, bf16[2304,1024]{1,0:T(8,128)(2,1)} %param.13), kind=kOutput, calls=%fused_computation.21 | convolution fusion | flops 302055424 | bytes 5144576 | tf_op jit(solution)/shard_map/dot_general | solution.py:54
  10.1 0.1 all_gather_reshape.3
  10.2 12.5 %all_gather.3 = bf16[4,64,2,2,256]{4,1,3,2,0:T(8,128)(2,1)} all-gather(bf16[1,64,2,2,256]{4,1,3,2,0:T(8,128)(2,1)S(1)} %copy.28), channel_id=1, replica_groups=mesh['dp'=1,'heads'=2,'ctx'=4] {'ctx'}, dimensions={0}, use_global_device_ids=true | all-gather | bytes 655360 | tf_op jit(solution)/shard_map/all_gather | solution.py:57
  22.6 1.4 copy.29
  24.0 2.4 %copy.30 = bf16[1024,2,256]{2,0,1:T(8,128)(2,1)} copy(bf16[1024,2,256]{2,1,0:T(2,128)(2,1)} %param.18) | data formatting | bytes 2097152 | tf_op jit(solution)/shard_map/while | solution.py:58
  26.3 0.0 copy-start.3
  26.3 16.5 %while.12 = (s32[]{:T(128)}, f32[4,64,2,2,256]{4,1,3,2,0:T(8,128)}, f32[4,64,2,2]{1,3,2,0:T(2,128)S(1)}, bf16[4,64,2,2,256]{4,1,3,2,0:T(8,128)(2,1)}, bf16[1024,...) while((s32[]{:T(128)}, f32[4,64,2,2,256]{4,1,3,2,0:T(8,128)}, ...), condition=%wide.region_3.4_spmd, body=%wide.region_0.3_spmd.sunk | while | flops 270073600 | bytes 5648465 | solution.py:58
  26.3 1.5 %fusion.75 = (f32[64,2,2]{0,2,1:T(2,128)S(1)}, f32[64,2,2,1024]{3,0,2,1:T(8,128)S(1)}) fusion(bf16[1024,2,256]{2,0,1:T(8,128)(2,1)S(1)} %get-tuple-element.141, bf16[4,64,2,2,256]{4,1,3,2,0:T(8,128)(2,1)} %get-tuple-element.140, s32[]{:T(128)} %get-tuple-element.130), kind=kOutput, calls=%fused_computation.50.clone.1 | convolution fusion | flops 134741760 | bytes 2229760 | tf_op jit(solution)/shard_map/while/body/eval_jaxpr/bkgd,pkd->bkgp/dot_general | solution.py:10
  27.8 0.3 fusion.76
  28.2 2.3 %fusion.77 = f32[4,64,2,2,256]{4,1,3,2,0:T(8,128)} fusion(f32[4,64,2,2,256]{4,1,3,2,0:T(8,128)} %get-tuple-element.131, s32[]{:T(128)} %get-tuple-element.130, bf16[1024,2,256]{2,0,1:T(8,128)(2,1)} %get-tuple-element.142, f32[64,2,2,1024]{3,0,2,1:T(8,128)S(1)} %get-tuple-element.121, f32[64,2,2]{0,2,1:T(2,128)S(1)} %get-tuple-element.122, ...), kind=kOutput, calls=%fused_computation.5.clone.1 | convolution fusion | flops 134807552 | bytes 2361856 | tf_op jit(solution)/shard_map/while/body/eval_jaxpr/bkgp,pkd->bkgd/dot_general | solution.py:14
  30.5 1.5 %fusion.75 = (f32[64,2,2]{0,2,1:T(2,128)S(1)}, f32[64,2,2,1024]{3,0,2,1:T(8,128)S(1)}) fusion(bf16[1024,2,256]{2,0,1:T(8,128)(2,1)S(1)} %get-tuple-element.141, bf16[4,64,2,2,256]{4,1,3,2,0:T(8,128)(2,1)} %get-tuple-element.140, s32[]{:T(128)} %get-tuple-element.130), kind=kOutput, calls=%fused_computation.50.clone.1 | convolution fusion | flops 134741760 | bytes 2229760 | tf_op jit(solution)/shard_map/while/body/eval_jaxpr/bkgd,pkd->bkgp/dot_general | solution.py:10
  31.9 0.3 fusion.76
  32.3 2.3 %fusion.77 = f32[4,64,2,2,256]{4,1,3,2,0:T(8,128)} fusion(f32[4,64,2,2,256]{4,1,3,2,0:T(8,128)} %get-tuple-element.131, s32[]{:T(128)} %get-tuple-element.130, bf16[1024,2,256]{2,0,1:T(8,128)(2,1)} %get-tuple-element.142, f32[64,2,2,1024]{3,0,2,1:T(8,128)S(1)} %get-tuple-element.121, f32[64,2,2]{0,2,1:T(2,128)S(1)} %get-tuple-element.122, ...), kind=kOutput, calls=%fused_computation.5.clone.1 | convolution fusion | flops 134807552 | bytes 2361856 | tf_op jit(solution)/shard_map/while/body/eval_jaxpr/bkgp,pkd->bkgd/dot_general | solution.py:14
  34.6 1.5 %fusion.75 = (f32[64,2,2]{0,2,1:T(2,128)S(1)}, f32[64,2,2,1024]{3,0,2,1:T(8,128)S(1)}) fusion(bf16[1024,2,256]{2,0,1:T(8,128)(2,1)S(1)} %get-tuple-element.141, bf16[4,64,2,2,256]{4,1,3,2,0:T(8,128)(2,1)} %get-tuple-element.140, s32[]{:T(128)} %get-tuple-element.130), kind=kOutput, calls=%fused_computation.50.clone.1 | convolution fusion | flops 134741760 | bytes 2229760 | tf_op jit(solution)/shard_map/while/body/eval_jaxpr/bkgd,pkd->bkgp/dot_general | solution.py:10
  36.1 0.3 fusion.76
  36.4 2.3 %fusion.77 = f32[4,64,2,2,256]{4,1,3,2,0:T(8,128)} fusion(f32[4,64,2,2,256]{4,1,3,2,0:T(8,128)} %get-tuple-element.131, s32[]{:T(128)} %get-tuple-element.130, bf16[1024,2,256]{2,0,1:T(8,128)(2,1)} %get-tuple-element.142, f32[64,2,2,1024]{3,0,2,1:T(8,128)S(1)} %get-tuple-element.121, f32[64,2,2]{0,2,1:T(2,128)S(1)} %get-tuple-element.122, ...), kind=kOutput, calls=%fused_computation.5.clone.1 | convolution fusion | flops 134807552 | bytes 2361856 | tf_op jit(solution)/shard_map/while/body/eval_jaxpr/bkgp,pkd->bkgd/dot_general | solution.py:14
  38.7 1.5 %fusion.75 = (f32[64,2,2]{0,2,1:T(2,128)S(1)}, f32[64,2,2,1024]{3,0,2,1:T(8,128)S(1)}) fusion(bf16[1024,2,256]{2,0,1:T(8,128)(2,1)S(1)} %get-tuple-element.141, bf16[4,64,2,2,256]{4,1,3,2,0:T(8,128)(2,1)} %get-tuple-element.140, s32[]{:T(128)} %get-tuple-element.130), kind=kOutput, calls=%fused_computation.50.clone.1 | convolution fusion | flops 134741760 | bytes 2229760 | tf_op jit(solution)/shard_map/while/body/eval_jaxpr/bkgd,pkd->bkgp/dot_general | solution.py:10
  40.2 0.3 fusion.76
  40.5 2.3 %fusion.77 = f32[4,64,2,2,256]{4,1,3,2,0:T(8,128)} fusion(f32[4,64,2,2,256]{4,1,3,2,0:T(8,128)} %get-tuple-element.131, s32[]{:T(128)} %get-tuple-element.130, bf16[1024,2,256]{2,0,1:T(8,128)(2,1)} %get-tuple-element.142, f32[64,2,2,1024]{3,0,2,1:T(8,128)S(1)} %get-tuple-element.121, f32[64,2,2]{0,2,1:T(2,128)S(1)} %get-tuple-element.122, ...), kind=kOutput, calls=%fused_computation.5.clone.1 | convolution fusion | flops 134807552 | bytes 2361856 | tf_op jit(solution)/shard_map/while/body/eval_jaxpr/bkgp,pkd->bkgd/dot_general | solution.py:14
  42.8 0.7 reshape.66
  43.5 3.2 %all-to-all-start = ((f32[4,1,256]{2,1,0:T(1,128)}), f32[4,1,256]{2,1,0:T(1,128)S(1)}, u32[]{:S(2)}, u32[]{:S(2)}) async-start(f32[4,1,256]{2,1,0:T(1,128)} %reshape.66), calls=%async_computation | async-start | bytes 8192 | tf_op jit(solution)/shard_map/all_to_all | solution.py:60
  46.7 0.1 reshape.55
  46.8 0.0 copy-done.3
  46.8 0.1 iota_compare_fusion
  46.9 0.0 copy-start.2
  46.9 14.6 %fusion.54 = (f32[64,2,2]{2,1,0:T(2,128)S(1)}, f32[64,2,2,512]{3,2,1,0:T(2,128)S(1)}) fusion(bf16[64,2,2,256]{3,2,1,0:T(2,128)(2,1)S(1)} %reshape.55, bf16[64,512,2,256]{3,2,1,0:T(2,128)(2,1)} %param.19, pred[64,512]{1,0:T(8,128)(4,1)S(1)} %iota_compare_fusion), kind=kOutput, calls=%fused_computation.51 | convolution fusion | flops 67501824 | bytes 34243584 | tf_op jit(solution)/shard_map/bkgd,bskd->bkgs/dot_general | solution.py:20
  61.5 0.1 copy.32
  61.6 0.0 copy-done
  61.6 0.0 copy-done.2
  61.6 0.5 convolution_convert_fusion.2
  62.2 0.3 fusion.55
  62.5 0.1 copy.44
  62.6 0.1 copy.33
  62.7 2.2 %fusion.23 = f32[64,512]{1,0:T(8,128)S(1)} fusion(bf16[64,2304]{1,0:T(8,128)(2,1)S(1)} %copy-done.2, bf16[2304,512]{1,0:T(8,128)(2,1)} %param.15), kind=kOutput, calls=%fused_computation.25 | convolution fusion | flops 151060480 | bytes 2785280 | tf_op jit(solution)/shard_map/dot_general | solution.py:56
  64.9 0.7 fusion.43
  65.6 0.1 copy.34
  65.7 0.7 copy.37
  66.4 0.7 reshape.59
  67.1 0.0 all-to-all-done
  67.1 3.5 %all-to-all-start.1 = ((f32[4,64,2,2,256]{4,1,3,2,0:T(8,128)}), f32[4,64,2,2,256]{4,1,3,2,0:T(8,128)S(1)}, u32[]{:S(2)}, u32[]{:S(2)}) async-start(f32[4,64,2,2,256]{4,1,3,2,0:T(8,128)} %get-tuple-element.39), calls=%async_computation.1 | async-start | bytes 2097152 | tf_op jit(solution)/shard_map/all_to_all | solution.py:59
  70.7 0.2 all-reduce.2.cloned.1.call-start
  70.9 0.6 broadcast.25
  71.5 0.7 reduce
  72.2 0.1 reshape.67
  72.3 0.7 copy.38
  73.1 0.7 copy.35
  73.8 0.7 copy.40
  74.6 10.5 %all-to-all-done.1 = f32[4,64,2,2,256]{4,1,3,2,0:T(8,128)S(1)} async-done(((f32[4,64,2,2,256]{4,1,3,2,0:T(8,128)}), f32[4,64,2,2,256]{4,1,3,2,0:T(8,128)S(1)}, u32[]{:S(2)}, u32[]{:S(2)}) %all-to-all-start.1) | async-done | bytes 1048608 | tf_op jit(solution)/shard_map/all_to_all | solution.py:59
  85.1 0.2 multiply_reduce_fusion
  85.3 0.0 copy-start.1
  85.3 16.0 %fusion.39 = bf16[64,2,2,256]{3,2,1,0:T(2,128)(2,1)} fusion(bf16[64,512,2,256]{3,2,1,0:T(2,128)(2,1)} %param.20, f32[64,2,2,512]{3,2,1,0:T(2,128)S(1)} %get-tuple-element.81, f32[64,2,2,256]{3,0,2,1:T(8,128)S(1)} %multiply_reduce_fusion, f32[64,2,2]{2,1,0:T(2,128)S(1)} %copy.33, f32[64,2,2]{2,1,0:T(2,128)} %copy.40, f32[64,2,2]{2,1,0:T(2,128)} %copy.38, ...), kind=kOutput, calls=%fused_computation.32 | convolution fusion | flops 67829760 | bytes 34608128 | tf_op jit(solution)/shard_map/bkgs,bskd->bkgd/dot_general | solution.py:29
  101.3 1.0 reshape.58
  102.3 4.1 %fusion.56 = f32[64,2304]{1,0:T(8,128)} fusion(bf16[64,1024]{1,0:T(8,128)(2,1)S(1)} %reshape.58, bf16[1024,2304]{1,0:T(8,128)(2,1)} %param.16), kind=kOutput, calls=%fused_computation.54 | convolution fusion | flops 301989888 | bytes 5439488 | tf_op jit(solution)/shard_map/dot_general | solution.py:64
  106.4 0.0 all-reduce.2.cloned.1.call-update
  106.4 24.7 %all-reduce.2.cloned.1.call-done = f32[64,2304]{1,0:T(8,128)} async-done(((f32[64,2304]{1,0:T(8,128)}), f32[64,2304]{1,0:T(8,128)}) %all-reduce.2.cloned.1.call-update) | async-done | bytes 589840 | tf_op jit(solution)/shard_map/psum | solution.py:65
  131.1 1.8 %add_convert_fusion = bf16[64,2304]{1,0:T(8,128)(2,1)} fusion(f32[64,2304]{1,0:T(8,128)} %all-reduce.2.cloned.1.call-done, bf16[64,2304]{1,0:T(8,128)(2,1)S(1)} %copy-done.2), kind=kLoop, calls=%fused_computation.33 | loop fusion | flops 442368 | bytes 1179648 | tf_op jit(solution)/shard_map/convert_element_type | solution.py:66
  133.0 0.0 copy-done.1
  (13 shorter events, 0.2 us)
Async XLA Ops:
  6.5 55.1 %copy-start = (bf16[2304,512]{1,0:T(8,128)(2,1)S(1)}, bf16[2304,512]{1,0:T(8,128)(2,1)}, u32[]{:S(2)}) copy-start(bf16[2304,512]{1,0:T(8,128)(2,1)} %param.14) | copy-start | bytes 7077892
  26.3 20.5 %copy-start.3 = (s32[64]{0:T(128)S(1)}, s32[64]{0:T(128)}, u32[]{:S(2)}) copy-start(s32[64]{0:T(128)} %param.21) | copy-start | bytes 772
  43.5 23.7 %all-to-all-start = ((f32[4,1,256]{2,1,0:T(1,128)}), f32[4,1,256]{2,1,0:T(1,128)S(1)}, u32[]{:S(2)}, u32[]{:S(2)}) async-start(f32[4,1,256]{2,1,0:T(1,128)} %reshape.66), calls=%async_computation | async-start | bytes 8192 | tf_op jit(solution)/shard_map/all_to_all | solution.py:60
  46.9 14.7 %copy-start.2 = (bf16[64,2304]{1,0:T(8,128)(2,1)S(1)}, bf16[64,2304]{1,0:T(8,128)(2,1)}, u32[]{:S(2)}) copy-start(bf16[64,2304]{1,0:T(8,128)(2,1)} %param.12) | copy-start | bytes 884740
  67.1 17.9 %all-to-all-start.1 = ((f32[4,64,2,2,256]{4,1,3,2,0:T(8,128)}), f32[4,64,2,2,256]{4,1,3,2,0:T(8,128)S(1)}, u32[]{:S(2)}, u32[]{:S(2)}) async-start(f32[4,64,2,2,256]{4,1,3,2,0:T(8,128)} %get-tuple-element.39), calls=%async_computation.1 | async-start | bytes 2097152 | tf_op jit(solution)/shard_map/all_to_all | solution.py:59
  70.7 60.5 %all-reduce.2.cloned.1.call-start = ((), (), s32[]{:S(2)}) async-start(), calls=%async_computation.2 | async-start | bytes 1179648 | tf_op jit(solution)/shard_map/psum | solution.py:65
  85.3 47.7 %copy-start.1 = (bf16[2304,512]{1,0:T(8,128)(2,1)S(1)}, bf16[2304,512]{1,0:T(8,128)(2,1)}, u32[]{:S(2)}) copy-start(bf16[2304,512]{1,0:T(8,128)(2,1)} %param.14) | copy-start | bytes 7077892
Sparse Core Ops, SparseCore 0:
  106.5 24.5 all-reduce.1
where the time goes:
time: 141 us; the launch traced here: 140 us
  matrix products  56.3 us (40%)
  waiting for transfers between devices  35.2 us (25%)
  between operations  13.6 us (10%)
  blocking collectives  12.5 us (9%)
  local copies, waits for them, and re-layouts  10.3 us (7%)
  starting transfers between devices  6.98 us (5%)
  other arithmetic  4.9 us (3%)
    psum x1, waiting for transfers between devices, local_step(): summed_y = lax.psum(partial_y, 'heads')  24.7 us
    dot_general x1, matrix products, suffix_state(): jnp.einsum('bkgs,bskd->bkgd', w_cached.astype(jnp.bfloat16), suf_v, prefe...  16 us
    dot_general x1, matrix products, suffix_state(): jnp.einsum('bkgd,bskd->bkgs', queries, suf_k, preferred_element_type=jnp....  14.6 us
    all_gather x1, blocking collectives, local_step(): all_queries = lax.all_gather(queries, 'ctx', axis=0)  12.5 us
    all_to_all x1, waiting for transfers between devices, local_step(): pre_out = lax.all_to_all(pre_out, 'ctx', 0, 0, tiled=True)  10.5 us
    dot_general x4, matrix products, prefix_state(): jnp.einsum('bkgp,pkd->bkgd', weights.astype(jnp.bfloat16), pre_v, preferr...  9.25 us
    dot_general x4, matrix products, prefix_state(): jnp.einsum('bkgd,pkd->bkgp', q_block, pre_k, preferred_element_type=jnp.f...  5.87 us
    dot_general x1, matrix products, local_step(): partial_y = jnp.dot(attended, w_out, preferred_element_type=jnp.float32)  4.08 us
  transfers between devices with their start and end apart: 3, of which 2 were waited for; matrix products, arithmetic and copies ran while one was open for 17% of the time, Pallas kernels for 0%

commit v1 on v0

v1 whole, which is shorter than its diff:
```python
import functools
import math
import jax
import jax.numpy as jnp
from jax import lax
from jax.experimental import pallas as pl
from jax.experimental.pallas import tpu as pltpu
from jax.sharding import PartitionSpec as P

F32 = jnp.float32
BF16 = jnp.bfloat16
NEG = -3.0e38
RING = 24
MESH = pl.DeviceIdType.MESH
CONTRACT_LAST = (((1,), (1,)), ((), ()))


def step_kernel(x_hbm, wq_hbm, wk_hbm, wv_hbm, wo_hbm, pk_hbm, pv_hbm, sk_hbm, sv_hbm, lens_ref, y_ref,
                x, wq, wk, wv, wo, pk, pv, pve, pvo, kring, vring, qs, qrecv, qrow, snew, vnew,
                tbuf, pbuf, opart, orecv, osuf, msuf, lsuf, att, yown, yrecv,
                wsem, ksem, vsem, qsend, qrecvs, osend, orecvs, ysend, yrecvs):
    nb, width = x.shape
    slots = sk_hbm.shape[1]
    hd = 256
    rows = 2 * slots
    prows = pk.shape[1]
    factor = hd ** -0.5 * math.log2(math.e)
    groups = 4
    gsz = nb // groups
    me = lax.axis_index('ctx')
    sib = me + 1 - 2 * lax.rem(me, 2)
    far = lax.rem(me + 2, 4)
    cross = lax.rem(sib + 2, 4)
    peers = (me, sib, far, cross)
    head = lax.axis_index('heads')

    sk = sk_hbm.reshape(nb, rows, hd)
    sv = sv_hbm.reshape(nb, rows, hd)
    pkr = pk_hbm.reshape(prows, hd)
    pvr = pv_hbm.reshape(prows, hd)

    weight_copies = [
        pltpu.make_async_copy(x_hbm, x, wsem.at[0]),
        pltpu.make_async_copy(wq_hbm, wq, wsem.at[1]),
        pltpu.make_async_copy(wk_hbm, wk, wsem.at[2]),
        pltpu.make_async_copy(wv_hbm, wv, wsem.at[3]),
        pltpu.make_async_copy(wo_hbm, wo, wsem.at[4]),
    ]
    pk_copies = [pltpu.make_async_copy(pkr.at[:, pl.ds(d * 128, 128)], pk.at[d], wsem.at[5]) for d in range(2)]
    pv_copies = [pltpu.make_async_copy(pvr.at[:, pl.ds(d * 128, 128)], pv.at[d], wsem.at[6]) for d in range(2)]

    def kcopies(i, slot):
        return [pltpu.make_async_copy(sk.at[i, :, pl.ds(d * 128, 128)], kring.at[slot, d], ksem.at[slot]) for d in range(2)]

    def vcopies(i, slot):
        return [pltpu.make_async_copy(sv.at[i, :, pl.ds(d * 128, 128)], vring.at[slot, d], vsem.at[slot]) for d in range(2)]

    def start(copies):
        for c in copies:
            c.start()

    def finish(copies):
        for c in copies:
            c.wait()

    start(weight_copies[:4])
    start(pk_copies)
    start(pv_copies)

    barrier = pltpu.get_barrier_semaphore()
    for peer in peers[1:]:
        pl.semaphore_signal(barrier, inc=1, device_id={'ctx': peer}, device_id_type=MESH)
    pl.semaphore_signal(barrier, inc=1, device_id={'heads': 1 - head}, device_id_type=MESH)
    pl.semaphore_wait(barrier, 4)

    weight_copies[0].wait()
    weight_copies[1].wait()
    q = jnp.dot(x[...], wq[...], preferred_element_type=F32).astype(BF16)
    for j in range(4):
        qs[pl.ds(j * nb, nb), :] = q[:, j * hd:(j + 1) * hd]
    qf = q.astype(F32)

    q_copies = [pltpu.make_async_remote_copy(src_ref=qs, dst_ref=qrecv.at[r - 1], send_sem=qsend.at[r - 1], recv_sem=qrecvs.at[r - 1],
                                             device_id={'ctx': peers[r]}, device_id_type=MESH) for r in (1, 2, 3)]
    q_copies[1].start()
    q_copies[2].start()
    q_copies[0].start()

    for i in range(RING):
        start(kcopies(i, i))
        start(vcopies(i, i))
    weight_copies[4].start()

    for j in range(4):
        for d in range(2):
            qrow[d, pl.ds(j, nb, stride=4), :] = qf[:, j * hd + d * 128:j * hd + (d + 1) * 128]

    weight_copies[2].wait()
    weight_copies[3].wait()
    kf = jnp.dot(x[...], wk[...], preferred_element_type=F32).astype(BF16).astype(F32)
    vnew[...] = jnp.dot(x[...], wv[...], preferred_element_type=F32).astype(BF16).astype(F32)
    for j in range(4):
        prod = qf[:, j * hd:(j + 1) * hd] * kf[:, (j // 2) * hd:(j // 2 + 1) * hd]
        snew[j] = jnp.broadcast_to(jnp.sum(prod, axis=1, keepdims=True), (nb, 128))

    finish(pv_copies)
    odd_row = lax.rem(lax.broadcasted_iota(jnp.int32, (prows, 128), 0), 2).astype(F32).astype(BF16)
    even_row = 1 - odd_row
    for d in range(2):
        pve[:, pl.ds(d * 128, 128)] = pv[d] * even_row
        pvo[:, pl.ds(d * 128, 128)] = pv[d] * odd_row
    finish(pk_copies)

    lane = lax.broadcasted_iota(jnp.int32, (nb, 128), 1)
    even128 = lax.rem(lax.broadcasted_iota(jnp.int32, (2 * nb, 128), 1), 2) == 0
    even256 = lax.rem(lax.broadcasted_iota(jnp.int32, (2 * nb, 256), 1), 2) == 0

    def prefix(r):
        qv = qs[...] if r == 0 else qrecv[r - 1]
        mx = None
        for n in range(prows // 256):
            kt = jnp.concatenate([pk[0, pl.ds(n * 256, 256), :], pk[1, pl.ds(n * 256, 256), :]], axis=1)
            s = lax.dot_general(qv, kt, CONTRACT_LAST, preferred_element_type=F32)
            t = jnp.where(even256, s[:2 * nb], s[2 * nb:])
            tbuf[:, pl.ds(n * 256, 256)] = t
            top = jnp.maximum(t[:, :128], t[:, 128:])
            mx = top if mx is None else jnp.maximum(mx, top)
        m_even = jnp.max(jnp.where(even128, mx, NEG), axis=1, keepdims=True)
        m_odd = jnp.max(jnp.where(even128, NEG, mx), axis=1, keepdims=True)
        mv = jnp.where(even128, m_even, m_odd)
        tot = None
        for n in range(prows // 128):
            p = jnp.exp2((tbuf[:, pl.ds(n * 128, 128)] - mv) * factor)
            tot = p if tot is None else tot + p
            pbuf[:, pl.ds(n * 128, 128)] = p.astype(BF16)
        l_even = jnp.sum(jnp.where(even128, tot, 0.0), axis=1, keepdims=True)
        l_odd = jnp.sum(jnp.where(even128, 0.0, tot), axis=1, keepdims=True)
        stats = jnp.zeros((nb, 128), F32)
        for h, (vals, m, l) in enumerate(((pve, m_even, l_even), (pvo, m_odd, l_odd))):
            o = jnp.dot(pbuf[...], vals[...], preferred_element_type=F32)
            for g in range(2):
                j = 2 * h + g
                opart[r, :, pl.ds(j * hd, hd)] = o[g * nb:(g + 1) * nb]
                stats = jnp.where(lane == 2 * j, m[g * nb:(g + 1) * nb], stats)
                stats = jnp.where(lane == 2 * j + 1, l[g * nb:(g + 1) * nb], stats)
        opart[r, :, pl.ds(4 * hd, 128)] = stats

    def o_copy(r, g):
        part = pl.ds(g * gsz, gsz)
        return pltpu.make_async_remote_copy(src_ref=opart.at[r, part], dst_ref=orecv.at[r - 1, part], send_sem=osend.at[r - 1, g],
                                            recv_sem=orecvs.at[r - 1, g], device_id={'ctx': peers[r]}, device_id_type=MESH)

    row8 = lax.broadcasted_iota(jnp.int32, (8, rows), 0)
    col = lax.broadcasted_iota(jnp.int32, (8, rows), 1)
    same_head = lax.rem(col, 2) == lax.rem(row8 // 2, 2)
    slot_of = jnp.where(same_head, col // 2, 1 << 20)
    first = row8 < 4
    first128 = lax.broadcasted_iota(jnp.int32, (8, 128), 0) < 4
    first256 = lax.broadcasted_iota(jnp.int32, (8, 256), 0) < 4

    def scores(i):
        at = pl.multiple_of(i * 4, 8)
        q8 = jnp.concatenate([qrow[0, pl.ds(at, 8), :], qrow[1, pl.ds(at, 8), :]], axis=1).astype(BF16)
        out = []
        for u in range(2):
            slot = lax.rem(i + u, RING)
            kk = jnp.concatenate([kring[slot, 0], kring[slot, 1]], axis=1)
            out.append(lax.dot_general(q8, kk, CONTRACT_LAST, preferred_element_type=F32))
        return jnp.where(first, out[0], out[1])

    def values(i, s):
        at = pl.multiple_of(i * 4, 8)
        ln = jnp.where(first128, lens_ref[i], lens_ref[i + 1])
        ln = jnp.concatenate([ln] * (rows // 128), axis=1)
        s = jnp.where(slot_of < ln, s, NEG)
        m = jnp.max(s, axis=1, keepdims=True)
        p = jnp.exp2((s - m) * factor)
        l = jnp.sum(p, axis=1, keepdims=True)
        pb = p.astype(BF16)
        out = []
        for u in range(2):
            slot = lax.rem(i + u, RING)
            vv = jnp.concatenate([vring[slot, 0], vring[slot, 1]], axis=1)
            out.append(jnp.dot(pb, vv, preferred_element_type=F32))
        o = jnp.where(first256, out[0], out[1])
        osuf[0, pl.ds(at, 8), :] = o[:, :128]
        osuf[1, pl.ds(at, 8), :] = o[:, 128:]
        msuf[pl.ds(at, 8), :] = jnp.broadcast_to(m, (8, 128))
        lsuf[pl.ds(at, 8), :] = jnp.broadcast_to(l, (8, 128))

    def suffix(lo, hi, per=4):
        refill = lo + RING < nb

        def wait_k(i):
            for u in range(per):
                finish(kcopies(i + u, lax.rem(i + u, RING)))

        def wait_v(i):
            for u in range(per):
                finish(vcopies(i + u, lax.rem(i + u, RING)))

        def fill(i):
            if refill:
                for u in range(per):
                    start(kcopies(i + u + RING, lax.rem(i + u, RING)))
                    start(vcopies(i + u + RING, lax.rem(i + u, RING)))

        def body(it, ss):
            i = lo + it * per
            wait_k(i + per)
            wait_v(i)
            nxt = tuple(scores(i + per + 2 * u) for u in range(per // 2))
            for u in range(per // 2):
                values(i + 2 * u, ss[u])
            fill(i)
            return nxt

        wait_k(lo)
        ss = tuple(scores(lo + 2 * u) for u in range(per // 2))
        ss = lax.fori_loop(0, (hi - lo) // per - 1, body, ss)
        last = hi - per
        wait_v(last)
        for u in range(per // 2):
            values(last + 2 * u, ss[u])
        fill(last)

    def y_copy(g):
        part = pl.ds(g * gsz, gsz)
        return pltpu.make_async_remote_copy(src_ref=yown.at[part], dst_ref=yrecv.at[part], send_sem=ysend.at[g], recv_sem=yrecvs.at[g],
                                            device_id={'heads': 1 - head}, device_id_type=MESH)

    def merge(g):
        for r in (1, 2, 3):
            o_copy(r, g).wait_recv()
        part = pl.ds(g * gsz, gsz)
        srcs = [opart.at[0], orecv.at[0], orecv.at[1], orecv.at[2]]
        for j in range(4):
            rows_j = pl.ds(g * gsz * 4 + j, gsz, stride=4)
            ms = [msuf[rows_j, :], snew[j, part, :]]
            for src in srcs:
                ms.append(jnp.broadcast_to(src[part, pl.ds(4 * hd + 2 * j, 1)], (gsz, 128)))
            top = functools.reduce(jnp.maximum, ms)
            ws = [jnp.exp2((m - top) * factor) for m in ms]
            den = ws[0] * lsuf[rows_j, :] + ws[1]
            for w, src in zip(ws[2:], srcs):
                den = den + w * src[part, pl.ds(4 * hd + 2 * j + 1, 1)]
            for d in range(2):
                at = j * hd + d * 128
                num = ws[0] * osuf[d, rows_j, :] + ws[1] * vnew[part, pl.ds((j // 2) * hd + d * 128, 128)]
                for w, src in zip(ws[2:], srcs):
                    num = num + w * src[part, pl.ds(at, 128)]
                att[:, pl.ds(at, 128)] = (num / den).astype(BF16)
        yown[part, :] = jnp.dot(att[...], wo[...], preferred_element_type=F32)
        y_copy(g).start()

    prefix(0)
    suffix(0, 8)
    q_copies[1].wait_recv()
    prefix(2)
    o_copy(2, 0).start()
    q_copies[2].wait_recv()
    prefix(3)
    o_copy(3, 0).start()
    for g in range(1, groups):
        o_copy(2, g).start()
        o_copy(3, g).start()
    q_copies[0].wait_recv()
    prefix(1)
    for g in range(groups):
        o_copy(1, g).start()
    suffix(8, 24)
    suffix(24, 40)
    weight_copies[4].wait()
    merge(0)
    merge(1)
    suffix(40, 64)
    merge(2)
    merge(3)
    for c in q_copies:
        c.wait_send()
    for r in (1, 2, 3):
        for g in range(groups):
            o_copy(r, g).wait_send()
    for g in range(groups):
        part = pl.ds(g * gsz, gsz)
        y_copy(g).wait()
        y_ref[part, :] = (x[part, :].astype(F32) + (yown[part, :] + yrecv[part, :])).astype(BF16)


def solution(mesh):
    row_spec = P(('dp', 'ctx'), None)
    col_spec = P(None, 'heads')
    pre_spec = P(('dp', 'ctx'), 'heads', None)
    suf_spec = P(('dp', 'ctx'), None, 'heads', None)

    def local_step(hidden, w_query, w_key, w_value, w_out, prefix_k, prefix_v, suffix_k, suffix_v, seq_lens):
        nb, width = hidden.shape
        qw = w_query.shape[1]
        kvw = w_key.shape[1]
        prows = 2 * prefix_k.shape[0]
        rows = 2 * suffix_k.shape[1]
        any_spec = pl.BlockSpec(memory_space=pl.ANY)
        dma = pltpu.SemaphoreType.DMA
        v = pltpu.VMEM
        return pl.pallas_call(
            step_kernel,
            out_shape=jax.ShapeDtypeStruct((nb, width), BF16),
            in_specs=[any_spec] * 9 + [pl.BlockSpec(memory_space=pltpu.SMEM)],
            out_specs=pl.BlockSpec(memory_space=pltpu.VMEM),
            scratch_shapes=[
                v((nb, width), BF16), v((width, qw), BF16), v((width, kvw), BF16), v((width, kvw), BF16), v((qw, width), BF16),
                v((2, prows, 128), BF16), v((2, prows, 128), BF16), v((prows, 256), BF16), v((prows, 256), BF16),
                v((RING, 2, rows, 128), BF16), v((RING, 2, rows, 128), BF16),
                v((4 * nb, 256), BF16), v((3, 4 * nb, 256), BF16), v((2, 4 * nb, 128), F32), v((4, nb, 128), F32), v((nb, kvw), F32),
                v((2 * nb, prows), F32), v((2 * nb, prows), BF16),
                v((4, nb, qw + 128), F32), v((3, nb, qw + 128), F32),
                v((2, 4 * nb, 128), F32), v((4 * nb, 128), F32), v((4 * nb, 128), F32), v((nb // 4, qw), BF16),
                v((nb, width), F32), v((nb, width), F32),
                dma((7,)), dma((RING,)), dma((RING,)), dma((3,)), dma((3,)), dma((3, 4)), dma((3, 4)), dma((4,)), dma((4,)),
            ],
            compiler_params=pltpu.CompilerParams(collective_id=0, has_side_effects=True, vmem_limit_bytes=60 * 1024 * 1024),
        )(hidden, w_query, w_key, w_value, w_out, prefix_k, prefix_v, suffix_k, suffix_v, seq_lens)

    return jax.shard_map(local_step, mesh=mesh, in_specs=(row_spec, col_spec, col_spec, col_spec, P('heads', None), pre_spec, pre_spec, suf_spec, suf_spec, P(('dp', 'ctx'))), out_specs=row_spec, check_vma=False)
```

time: 141 us -> 44.2 us (0.31)
  matrix products: 56.3 us -> 0 us
  Pallas kernels: 0 us -> 42.4 us
  waiting for transfers between devices: 35.2 us -> 0 us
  between operations: 13.6 us -> 0.01 us
  blocking collectives: 12.5 us -> 0 us
  local copies, waits for them, and re-layouts: 10.3 us -> 1.69 us
  starting transfers between devices: 6.98 us -> 0 us
  other arithmetic: 4.9 us -> 0 us
    dot_general x15 -> x0, matrix products: 56.3 us -> none  [the longest x1 16 us: suffix_state(): jnp.einsum('bkgs,bskd->bkgd', w_cached.astype(jnp.bfloat16), suf_v, prefe...]
    pallas_call x0 -> x1, Pallas kernels: none -> 42.4 us  [local_step(): pl.pallas_call(step_kernel, out_shape=jax.ShapeDtypeStruct((nb, width), B...]
    psum x1 -> x0, waiting for transfers between devices: 24.7 us -> none  [local_step(): summed_y = lax.psum(partial_y, 'heads')]
    all_gather x1 -> x0, blocking collectives: 12.5 us -> none  [local_step(): all_queries = lax.all_gather(queries, 'ctx', axis=0)]
    all_to_all x2 -> x0, waiting for transfers between devices: 10.5 us -> none  [the longest x1 10.5 us: local_step(): pre_out = lax.all_to_all(pre_out, 'ctx', 0, 0, tiled=True)]
    all_to_all x2 -> x0, starting transfers between devices: 6.76 us -> none  [the longest x1 3.52 us: local_step(): pre_out = lax.all_to_all(pre_out, 'ctx', 0, 0, tiled=True)]
    while x2 -> x0, local copies, waits for them, and re-layouts: 3.72 us -> none  [local_step(): lax.map(functools.partial(prefix_state, pre_k=prefix_k, pre_v=prefix_v),...]
    reduce_sum x7 -> x0, other arithmetic: 2.15 us -> none  [the longest x4 1.25 us: prefix_state(): weight_sum = jnp.sum(weights, axis=-1)]
  transfers between devices with their start and end apart: 3 -> 0, of which waited for: 2 -> 0; matrix products, arithmetic and copies ran while one was open for 17% -> 0% of each run, Pallas kernels for 0% -> 0%
where the time goes in v1:
time: 44.2 us; the launch traced here: 44.1 us
  Pallas kernels  42.4 us (96%)
  local copies, waits for them, and re-layouts  1.69 us (4%)
    pallas_call x1, Pallas kernels, local_step(): pl.pallas_call(step_kernel, out_shape=jax.ShapeDtypeStruct((nb, width), B...  42.4 us
    unnamed x1, local copies, waits for them, and re-layouts  1.69 us

profile of v1, /device:TPU:0, one launch (start us, length us, event | category | flops | bytes accessed | tf_op | source)
XLA Modules:
  0.0 44.1 jit_solution(1550286503740500556)
XLA Ops:
  0.0 42.4 %shard_map.100 = bf16[64,2304]{1,0:T(8,128)(2,1)} custom-call(bf16[64,2304]{1,0:T(8,128)(2,1)} %x_hbm.1, bf16[2304,1024]{1,0:T(8,128)(2,1)} %wq_hbm.1, bf16[2304,512]{1,0:T(8,128)(2,1)} %wk_hbm.1, bf16[2304,512]{1,0:T(8,128)(2,1)} %wv_hbm.1, bf16[1024,2304]{1,0:T(8,128)(2,1)} %wo_hbm.1, bf16[1024,2,256]{2,1,0:T(2,128)(2,1)} %pk_hbm.1, ...), custom_call_target="tpu_custom_call" | custom-call | tf_op jit(solution)/shard_map/pallas_call | solution.py:305
  42.4 1.7 %copy.12 = bf16[64,2304]{1,0:T(8,128)(2,1)} copy(bf16[64,2304]{1,0:T(8,128)(2,1)} %shard_map.100) | data formatting | bytes 589824

commit v2 on v1

v2 whole, which is shorter than its diff:
```python
import functools
import math
import jax
import jax.numpy as jnp
from jax import lax
from jax.experimental import pallas as pl
from jax.experimental.pallas import tpu as pltpu
from jax.sharding import PartitionSpec as P

F32 = jnp.float32
BF16 = jnp.bfloat16
NEG = -3.0e38
PER = 4
RING = 6
GROUPS = ((0, 16), (16, 40), (40, 56), (56, 64))
SPLIT = 3
MESH = pl.DeviceIdType.MESH
CONTRACT_LAST = (((1,), (1,)), ((), ()))


def step_kernel(x_hbm, wq_hbm, wk_hbm, wv_hbm, wo_hbm, pk_hbm, pv_hbm, sk_hbm, sv_hbm, lens_hbm, y_ref,
                x, wq, wk, wv, wo, pk, pv, pve, pvo, kring, vring, qs, qrecv, qrow, snew, vnew,
                tbuf, pbuf, opart, orecv, osuf, msuf, lsuf, att, yown, yrecv, yfin, lens_ref,
                wsem, ksem, vsem, psend, precv, qsend, qrecvs, osend, orecvs, ysend, yrecvs, fsend, frecv):
    nb, width = x.shape
    slots = sk_hbm.shape[1]
    hd = 256
    rows = 2 * slots
    prows = pk.shape[2]
    factor = hd ** -0.5 * math.log2(math.e)
    me = lax.axis_index('ctx')
    sib = me + 1 - 2 * lax.rem(me, 2)
    far = lax.rem(me + 2, 4)
    head = lax.axis_index('heads')

    sk = sk_hbm.reshape(nb, rows, hd)
    sv = sv_hbm.reshape(nb, rows, hd)
    pkr = pk_hbm.reshape(prows, hd)
    pvr = pv_hbm.reshape(prows, hd)

    third = width // 3
    x_copy = pltpu.make_async_copy(x_hbm, x, wsem.at[0])
    lens_copy = pltpu.make_async_copy(lens_hbm, lens_ref, wsem.at[9])
    wq_copies = [pltpu.make_async_copy(wq_hbm.at[pl.ds(c * third, third)], wq.at[pl.ds(c * third, third)], wsem.at[1 + c]) for c in range(3)]
    wk_copy = pltpu.make_async_copy(wk_hbm, wk, wsem.at[4])
    wv_copy = pltpu.make_async_copy(wv_hbm, wv, wsem.at[5])
    wo_copy = pltpu.make_async_copy(wo_hbm, wo, wsem.at[6])
    pk_copies = [pltpu.make_async_copy(pkr.at[:, pl.ds(d * 128, 128)], pk.at[0, d], wsem.at[7]) for d in range(2)]
    pv_copies = [pltpu.make_async_copy(pvr.at[:, pl.ds(d * 128, 128)], pv.at[0, d], wsem.at[8]) for d in range(2)]

    def to_sibling(buf, n):
        return pltpu.make_async_remote_copy(src_ref=buf.at[0], dst_ref=buf.at[1], send_sem=psend.at[n], recv_sem=precv.at[n],
                                            device_id={'ctx': sib}, device_id_type=MESH)

    pk_share = to_sibling(pk, 0)
    pv_share = to_sibling(pv, 1)

    def kcopies(n):
        slot = lax.rem(n, RING)
        return [pltpu.make_async_copy(sk.at[pl.ds(n * PER, PER), :, pl.ds(d * 128, 128)], kring.at[slot, d], ksem.at[slot]) for d in range(2)]

    def vcopies(n):
        slot = lax.rem(n, RING)
        return [pltpu.make_async_copy(sv.at[pl.ds(n * PER, PER), :, pl.ds(d * 128, 128)], vring.at[slot, d], vsem.at[slot]) for d in range(2)]

    def start(copies):
        for c in copies:
            c.start()

    def finish(copies):
        for c in copies:
            c.wait()

    x_copy.start()
    lens_copy.start()
    start(wq_copies)

    barrier = pltpu.get_barrier_semaphore()
    pl.semaphore_signal(barrier, inc=1, device_id={'ctx': sib}, device_id_type=MESH)
    pl.semaphore_signal(barrier, inc=1, device_id={'ctx': far}, device_id_type=MESH)
    pl.semaphore_signal(barrier, inc=1, device_id={'heads': 1 - head}, device_id_type=MESH)
    start(pk_copies)
    start(pv_copies)
    wk_copy.start()
    wv_copy.start()
    pl.semaphore_wait(barrier, 3)

    x_copy.wait()
    q = None
    for c in range(3):
        wq_copies[c].wait()
        if c == 2:
            start(kcopies(0))
            start(vcopies(0))
        piece = jnp.dot(x[:, pl.ds(c * third, third)], wq[pl.ds(c * third, third), :], preferred_element_type=F32)
        q = piece if q is None else q + piece
    q = q.astype(BF16)
    for j in range(4):
        qs[pl.ds(j * nb, nb), :] = q[:, j * hd:(j + 1) * hd]
    qf = q.astype(F32)

    q_copy = pltpu.make_async_remote_copy(src_ref=qs, dst_ref=qrecv, send_sem=qsend.at[0], recv_sem=qrecvs.at[0],
                                          device_id={'ctx': far}, device_id_type=MESH)
    q_copy.start()
    finish(pk_copies)
    pk_share.start()
    finish(pv_copies)
    pv_share.start()

    for i in range(1, RING):
        start(kcopies(i))
        start(vcopies(i))
    wo_copy.start()

    for j in range(4):
        for d in range(2):
            qrow[d, pl.ds(j, nb, stride=4), :] = qf[:, j * hd + d * 128:j * hd + (d + 1) * 128]

    wk_copy.wait()
    wv_copy.wait()
    kf = jnp.dot(x[...], wk[...], preferred_element_type=F32).astype(BF16).astype(F32)
    vnew[...] = jnp.dot(x[...], wv[...], preferred_element_type=F32).astype(BF16).astype(F32)
    for j in range(4):
        prod = qf[:, j * hd:(j + 1) * hd] * kf[:, (j // 2) * hd:(j // 2 + 1) * hd]
        snew[j] = jnp.broadcast_to(jnp.sum(prod, axis=1, keepdims=True), (nb, 128))

    odd_row = lax.rem(lax.broadcasted_iota(jnp.int32, (prows, 128), 0), 2).astype(F32).astype(BF16)
    even_row = 1 - odd_row

    def split_values(c):
        for d in range(2):
            pve[pl.ds(c * prows, prows), pl.ds(d * 128, 128)] = pv[c, d] * even_row
            pvo[pl.ds(c * prows, prows), pl.ds(d * 128, 128)] = pv[c, d] * odd_row

    split_values(0)

    lane = lax.broadcasted_iota(jnp.int32, (nb, 128), 1)
    even128 = lax.rem(lax.broadcasted_iota(jnp.int32, (2 * nb, 128), 1), 2) == 0
    even256 = lax.rem(lax.broadcasted_iota(jnp.int32, (2 * nb, 256), 1), 2) == 0

    def prefix(r):
        qv = qrecv[...] if r else qs[...]
        mx = None
        for n in range(2 * prows // 256):
            c, at = divmod(n * 256, prows)
            kt = jnp.concatenate([pk[c, 0, pl.ds(at, 256), :], pk[c, 1, pl.ds(at, 256), :]], axis=1)
            s = lax.dot_general(qv, kt, CONTRACT_LAST, preferred_element_type=F32)
            t = jnp.where(even256, s[:2 * nb], s[2 * nb:])
            tbuf[:, pl.ds(n * 256, 256)] = t
            top = jnp.maximum(t[:, :128], t[:, 128:])
            mx = top if mx is None else jnp.maximum(mx, top)
        m_even = jnp.max(jnp.where(even128, mx, NEG), axis=1, keepdims=True)
        m_odd = jnp.max(jnp.where(even128, NEG, mx), axis=1, keepdims=True)
        mv = jnp.where(even128, m_even, m_odd)
        tot = None
        for n in range(2 * prows // 128):
            p = jnp.exp2((tbuf[:, pl.ds(n * 128, 128)] - mv) * factor)
            tot = p if tot is None else tot + p
            pbuf[:, pl.ds(n * 128, 128)] = p.astype(BF16)
        l_even = jnp.sum(jnp.where(even128, tot, 0.0), axis=1, keepdims=True)
        l_odd = jnp.sum(jnp.where(even128, 0.0, tot), axis=1, keepdims=True)
        stats = jnp.zeros((nb, 128), F32)
        for h, (vals, m, l) in enumerate(((pve, m_even, l_even), (pvo, m_odd, l_odd))):
            o = jnp.dot(pbuf[...], vals[...], preferred_element_type=F32)
            for g in range(2):
                j = 2 * h + g
                opart[r, :, pl.ds(j * hd, hd)] = o[g * nb:(g + 1) * nb]
                stats = jnp.where(lane == 2 * j, m[g * nb:(g + 1) * nb], stats)
                stats = jnp.where(lane == 2 * j + 1, l[g * nb:(g + 1) * nb], stats)
        opart[r, :, pl.ds(4 * hd, 128)] = stats

    def o_copy(g):
        lo, hi = GROUPS[g]
        part = pl.ds(lo, hi - lo)
        return pltpu.make_async_remote_copy(src_ref=opart.at[1, part], dst_ref=orecv.at[part], send_sem=osend.at[g],
                                            recv_sem=orecvs.at[g], device_id={'ctx': far}, device_id_type=MESH)

    row8 = lax.broadcasted_iota(jnp.int32, (8, rows), 0)
    col = lax.broadcasted_iota(jnp.int32, (8, rows), 1)
    same_head = lax.rem(col, 2) == lax.rem(row8 // 2, 2)
    slot_of = jnp.where(same_head, col // 2, 1 << 20)
    first = row8 < 4
    first128 = lax.broadcasted_iota(jnp.int32, (8, 128), 0) < 4
    first256 = lax.broadcasted_iota(jnp.int32, (8, 256), 0) < 4

    def scores(n, pair):
        at = pl.multiple_of((n * PER + 2 * pair) * 4, 8)
        slot = lax.rem(n, RING)
        q8 = jnp.concatenate([qrow[0, pl.ds(at, 8), :], qrow[1, pl.ds(at, 8), :]], axis=1).astype(BF16)
        out = []
        for u in (2 * pair, 2 * pair + 1):
            kk = jnp.concatenate([kring[slot, 0, u], kring[slot, 1, u]], axis=1)
            out.append(lax.dot_general(q8, kk, CONTRACT_LAST, preferred_element_type=F32))
        return jnp.where(first, out[0], out[1])

    def values(n, pair, s):
        i = n * PER + 2 * pair
        at = pl.multiple_of(i * 4, 8)
        slot = lax.rem(n, RING)
        ln = jnp.where(first128, lens_ref[i], lens_ref[i + 1])
        ln = jnp.concatenate([ln] * (rows // 128), axis=1)
        s = jnp.where(slot_of < ln, s, NEG)
        m = jnp.max(s, axis=1, keepdims=True)
        p = jnp.exp2((s - m) * factor)
        l = jnp.sum(p, axis=1, keepdims=True)
        pb = p.astype(BF16)
        out = []
        for u in (2 * pair, 2 * pair + 1):
            vv = jnp.concatenate([vring[slot, 0, u], vring[slot, 1, u]], axis=1)
            out.append(jnp.dot(pb, vv, preferred_element_type=F32))
        o = jnp.where(first256, out[0], out[1])
        osuf[0, pl.ds(at, 8), :] = o[:, :128]
        osuf[1, pl.ds(at, 8), :] = o[:, 128:]
        msuf[pl.ds(at, 8), :] = jnp.broadcast_to(m, (8, 128))
        lsuf[pl.ds(at, 8), :] = jnp.broadcast_to(l, (8, 128))

    pairs = range(PER // 2)
    blocks = nb // PER

    def first_scores():
        finish(kcopies(0))
        return tuple(scores(0, p) for p in pairs)

    def suffix(lo, hi, ss):
        lo, hi = lo // PER, hi // PER
        refill = hi + RING <= blocks
        assert refill or lo + RING >= blocks

        def body(n, ss):
            if refill:
                start(kcopies(n + RING))
            finish(kcopies(n + 1))
            finish(vcopies(n))
            nxt = tuple(scores(n + 1, p) for p in pairs)
            for p in pairs:
                values(n, p, ss[p])
            if refill:
                start(vcopies(n + RING))
            return nxt

        if hi < blocks:
            return lax.fori_loop(lo, hi, body, ss)
        ss = lax.fori_loop(lo, hi - 1, body, ss)
        finish(vcopies(hi - 1))
        for p in pairs:
            values(hi - 1, p, ss[p])

    half = width // 2
    mine = pl.ds(pl.multiple_of(head * half, 128), half)
    other = pl.ds(pl.multiple_of((1 - head) * half, 128), half)

    def y_copy(g):
        lo, hi = GROUPS[g]
        part = (pl.ds(lo, hi - lo), other if g < SPLIT else slice(None))
        return pltpu.make_async_remote_copy(src_ref=yown.at[part], dst_ref=yrecv.at[part], send_sem=ysend.at[g], recv_sem=yrecvs.at[g],
                                            device_id={'heads': 1 - head}, device_id_type=MESH)

    def f_copy(g):
        lo, hi = GROUPS[g]
        part = (pl.ds(lo, hi - lo), mine)
        return pltpu.make_async_remote_copy(src_ref=yfin.at[part], dst_ref=yfin.at[part], send_sem=fsend.at[g], recv_sem=frecv.at[g],
                                            device_id={'heads': 1 - head}, device_id_type=MESH)

    def finalize(g):
        y_copy(g).wait_recv()
        lo, hi = GROUPS[g]
        part = (pl.ds(lo, hi - lo), mine)
        yfin[part] = (x[part].astype(F32) + (yown[part] + yrecv[part])).astype(BF16)
        f_copy(g).start()

    def merge(g):
        o_copy(g).wait_recv()
        lo, hi = GROUPS[g]
        gsz = hi - lo
        part = pl.ds(lo, gsz)
        srcs = [opart.at[0], orecv]
        for j in range(4):
            rows_j = pl.ds(lo * 4 + j, gsz, stride=4)
            ms = [msuf[rows_j, :], snew[j, part, :]]
            for src in srcs:
                ms.append(jnp.broadcast_to(src[part, pl.ds(4 * hd + 2 * j, 1)], (gsz, 128)))
            top = functools.reduce(jnp.maximum, ms)
            ws = [jnp.exp2((m - top) * factor) for m in ms]
            den = ws[0] * lsuf[rows_j, :] + ws[1]
            for w, src in zip(ws[2:], srcs):
                den = den + w * src[part, pl.ds(4 * hd + 2 * j + 1, 1)]
            for d in range(2):
                at = j * hd + d * 128
                num = ws[0] * osuf[d, rows_j, :] + ws[1] * vnew[part, pl.ds((j // 2) * hd + d * 128, 128)]
                for w, src in zip(ws[2:], srcs):
                    num = num + w * src[part, pl.ds(at, 128)]
                att[pl.ds(0, gsz), pl.ds(at, 128)] = (num / den).astype(BF16)
        yown[part, :] = jnp.dot(att[pl.ds(0, gsz), :], wo[...], preferred_element_type=F32)
        y_copy(g).start()

    lens_copy.wait()
    ss = first_scores()
    ss = suffix(0, 8, ss)
    pv_share.wait_recv()
    split_values(1)
    pk_share.wait_recv()
    prefix(0)
    ss = suffix(8, 16, ss)
    q_copy.wait_recv()
    prefix(1)
    for g in range(len(GROUPS)):
        o_copy(g).start()
    ss = suffix(16, 40, ss)
    wo_copy.wait()
    merge(0)
    ss = suffix(40, 48, ss)
    merge(1)
    finalize(0)
    ss = suffix(48, 56, ss)
    merge(2)
    finalize(1)
    suffix(56, 64, ss)
    merge(3)
    finalize(2)
    q_copy.wait_send()
    pk_share.wait_send()
    pv_share.wait_send()
    for g, (lo, hi) in enumerate(GROUPS):
        o_copy(g).wait_send()
        y_copy(g).wait_send()
        part = pl.ds(lo, hi - lo)
        if g < SPLIT:
            f_copy(g).wait()
            y_ref[part, :] = yfin[part, :]
        else:
            y_copy(g).wait_recv()
            y_ref[part, :] = (x[part, :].astype(F32) + (yown[part, :] + yrecv[part, :])).astype(BF16)


def solution(mesh):
    row_spec = P(('dp', 'ctx'), None)
    col_spec = P(None, 'heads')
    pre_spec = P(('dp', 'ctx'), 'heads', None)
    suf_spec = P(('dp', 'ctx'), None, 'heads', None)

    def local_step(hidden, w_query, w_key, w_value, w_out, prefix_k, prefix_v, suffix_k, suffix_v, seq_lens):
        nb, width = hidden.shape
        qw = w_query.shape[1]
        kvw = w_key.shape[1]
        prows = 2 * prefix_k.shape[0]
        rows = 2 * suffix_k.shape[1]
        hbm_spec = pl.BlockSpec(memory_space=pltpu.HBM)
        dma = pltpu.SemaphoreType.DMA
        v = pltpu.VMEM
        return pl.pallas_call(
            step_kernel,
            out_shape=jax.ShapeDtypeStruct((nb, width), BF16),
            in_specs=[hbm_spec] * 10,
            out_specs=pl.BlockSpec(memory_space=pltpu.VMEM),
            scratch_shapes=[
                v((nb, width), BF16), v((width, qw), BF16), v((width, kvw), BF16), v((width, kvw), BF16), v((qw, width), BF16),
                v((2, 2, prows, 128), BF16), v((2, 2, prows, 128), BF16), v((2 * prows, 256), BF16), v((2 * prows, 256), BF16),
                v((RING, 2, PER, rows, 128), BF16), v((RING, 2, PER, rows, 128), BF16),
                v((4 * nb, 256), BF16), v((4 * nb, 256), BF16), v((2, 4 * nb, 128), F32), v((4, nb, 128), F32), v((nb, kvw), F32),
                v((2 * nb, 2 * prows), F32), v((2 * nb, 2 * prows), BF16),
                v((2, nb, qw + 128), F32), v((nb, qw + 128), F32),
                v((2, 4 * nb, 128), F32), v((4 * nb, 128), F32), v((4 * nb, 128), F32), v((nb // 2, qw), BF16),
                v((nb, width), F32), v((nb, width), F32), v((nb, width), BF16), pltpu.SMEM((nb,), jnp.int32),
                dma((10,)), dma((RING,)), dma((RING,)), dma((2,)), dma((2,)), dma((1,)), dma((1,)), dma((4,)), dma((4,)), dma((4,)), dma((4,)), dma((4,)), dma((4,)),
            ],
            compiler_params=pltpu.CompilerParams(collective_id=0, has_side_effects=True, vmem_limit_bytes=60 * 1024 * 1024),
        )(hidden, w_query, w_key, w_value, w_out, prefix_k, prefix_v, suffix_k, suffix_v, seq_lens)

    return jax.shard_map(local_step, mesh=mesh, in_specs=(row_spec, col_spec, col_spec, col_spec, P('heads', None), pre_spec, pre_spec, suf_spec, suf_spec, P(('dp', 'ctx'))), out_specs=row_spec, check_vma=False)
```

time: 44.2 us -> 39.4 us (0.89)
  Pallas kernels: 42.4 us -> 37.6 us
    pallas_call x1, Pallas kernels: 42.4 us -> 37.6 us  [local_step(): pl.pallas_call(step_kernel, out_shape=jax.ShapeDtypeStruct((nb, width), B...]
where the time goes in v2:
time: 39.4 us; the launch traced here: 39.3 us
  Pallas kernels  37.6 us (95%)
  local copies, waits for them, and re-layouts  1.69 us (4%)
    pallas_call x1, Pallas kernels, local_step(): pl.pallas_call(step_kernel, out_shape=jax.ShapeDtypeStruct((nb, width), B...  37.6 us
    unnamed x1, local copies, waits for them, and re-layouts  1.69 us

profile of v2, /device:TPU:0, one launch (start us, length us, event | category | flops | bytes accessed | tf_op | source)
XLA Modules:
  0.0 39.3 jit_solution(6921399528463510944)
XLA Ops:
  0.0 37.6 %shard_map.100 = bf16[64,2304]{1,0:T(8,128)(2,1)} custom-call(bf16[64,2304]{1,0:T(8,128)(2,1)} %x_hbm.1, bf16[2304,1024]{1,0:T(8,128)(2,1)} %wq_hbm.1, bf16[2304,512]{1,0:T(8,128)(2,1)} %wk_hbm.1, bf16[2304,512]{1,0:T(8,128)(2,1)} %wv_hbm.1, bf16[1024,2304]{1,0:T(8,128)(2,1)} %wo_hbm.1, bf16[1024,2,256]{2,1,0:T(2,128)(2,1)} %pk_hbm.1, ...), custom_call_target="tpu_custom_call" | custom-call | tf_op jit(solution)/shard_map/pallas_call | solution.py:350
  37.6 1.7 %copy.12 = bf16[64,2304]{1,0:T(8,128)(2,1)} copy(bf16[64,2304]{1,0:T(8,128)(2,1)} %shard_map.100) | data formatting | bytes 589824

commit v3 on v2

--- a/solution.py
+++ b/solution.py
@@ -300,12 +300,12 @@
     split_values(1)
     pk_share.wait_recv()
     prefix(0)
-    ss = suffix(8, 16, ss)
+    ss = suffix(8, 24, ss)
     q_copy.wait_recv()
     prefix(1)
     for g in range(len(GROUPS)):
         o_copy(g).start()
-    ss = suffix(16, 40, ss)
+    ss = suffix(24, 40, ss)
     wo_copy.wait()
     merge(0)
     ss = suffix(40, 48, ss)

time: 39.4 us -> 40.4 us (1.025)
  Pallas kernels: 37.6 us -> 38.6 us
    pallas_call x1, Pallas kernels: 37.6 us -> 38.6 us  [local_step(): pl.pallas_call(step_kernel, out_shape=jax.ShapeDtypeStruct((nb, width), B...]
where the time goes in v3:
time: 40.4 us; the launch traced here: 40.3 us
  Pallas kernels  38.6 us (96%)
  local copies, waits for them, and re-layouts  1.69 us (4%)
    pallas_call x1, Pallas kernels, local_step(): pl.pallas_call(step_kernel, out_shape=jax.ShapeDtypeStruct((nb, width), B...  38.6 us
    unnamed x1, local copies, waits for them, and re-layouts  1.69 us

profile of v3, /device:TPU:0, one launch (start us, length us, event | category | flops | bytes accessed | tf_op | source)
XLA Modules:
  0.0 40.3 jit_solution(17093580259405750081)
XLA Ops:
  0.0 38.6 %shard_map.100 = bf16[64,2304]{1,0:T(8,128)(2,1)} custom-call(bf16[64,2304]{1,0:T(8,128)(2,1)} %x_hbm.1, bf16[2304,1024]{1,0:T(8,128)(2,1)} %wq_hbm.1, bf16[2304,512]{1,0:T(8,128)(2,1)} %wk_hbm.1, bf16[2304,512]{1,0:T(8,128)(2,1)} %wv_hbm.1, bf16[1024,2304]{1,0:T(8,128)(2,1)} %wo_hbm.1, bf16[1024,2,256]{2,1,0:T(2,128)(2,1)} %pk_hbm.1, ...), custom_call_target="tpu_custom_call" | custom-call | tf_op jit(solution)/shard_map/pallas_call | solution.py:350
  38.6 1.7 %copy.12 = bf16[64,2304]{1,0:T(8,128)(2,1)} copy(bf16[64,2304]{1,0:T(8,128)(2,1)} %shard_map.100) | data formatting | bytes 589824
